TPU v7x, 256 devices: a whole 4x4x8 slice. The times are simulated.
256 devices in a mesh: tm: 64 (over z, y, x_lo), space: 4 (over x_hi, core).
Axes of the slice: x: 4 (x_hi: 2, x_lo: 2; x = x_hi * 2 + x_lo), y: 4, z: 8, core: 2. Of those that a mesh axis runs over, the one named last changes fastest.
Arguments:
- increments: float32 [64, 3, 512, 1024], P('tm', None, 'space'), may hold values from -6 to 6
- start_state: float32 [3, 512, 1024], P(None, 'space'), may hold values from -6 to 6
- depth: float32 [512, 1024], P('space'), may hold values from 0.5 to 1.5
- error_weight: float32 [3, 512, 1024], P(None, 'space'), may hold values from 0.25 to 1
- obs_index: int32 [64, 4096], P('tm'), may hold values from 0 to 1572863
- obs_count: int32 [64], P('tm'), may hold values from 1024 to 4096, as said below
- obs_value: float32 [64, 4096], P('tm'), may hold values from -6 to 6
- obs_weight: float32 [64, 4096], P('tm'), may hold values from 0.5 to 2
Outputs:
- analysis: float32 [64, 3, 512, 1024], P('tm', None, 'space')
- costs: float32 [2, 64], P(None, 'tm')
Inputs may be any that keep to these rules, and one draw needn't show every extreme that they name: Only the first obs_count entries of a subwindow's observation rows are live; some subwindow has all 4096 live.
All inputs are finite; a program needn't handle non-finite values.
Results may differ from a plain program's by a relative error of at most 0.0001.
Values sent between devices are 32-bit elements; how exact they have to be, the bound alone decides.
A program may use at most 128 MiB of HBM per device.

v0:
```python
import functools
import math

import jax
import jax.numpy as jnp
from jax import lax
from jax.experimental import pallas as pl
from jax.experimental.pallas import tpu as pltpu
from jax.sharding import PartitionSpec as P

STEPS = 6
ITERS = 2
COURANT = 0.35
HALF = 0.5 * COURANT
CORIOLIS_MAX = 0.2
STEP_SIZE = 0.2
HALO = 2 * STEPS
TOP = 16
BLK = 8
STREAMS = 4
ORDER = (0, 3, 1, 2)
MESH = pl.DeviceIdType.MESH


def dlon(f):
    lane = lax.broadcasted_iota(jnp.int32, f.shape, 2)
    g = pltpu.roll(f, 127, axis=2)
    g = jnp.where(lane == 127, pltpu.roll(g, 7, axis=1), g)
    m = pltpu.roll(f, 1, axis=2)
    m = jnp.where(lane == 0, pltpu.roll(m, 1, axis=1), m)
    return g - m


def row_blocks(rows):
    low, high = TOP - HALO, TOP + rows + HALO
    return [(r, min(BLK, high - r)) for r in range(low, high, BLK)]


def edge_rows(T, rows, keep_top, keep_bottom):
    T[2, TOP - 1] = T[2, TOP - 1] * keep_top
    T[2, TOP + rows] = T[2, TOP + rows] * keep_bottom


def forward(T, D, F, rows, keep_top, keep_bottom):
    def step(_, carry):
        for r, n in row_blocks(rows):
            du = D[r : r + n] * T[0, r : r + n]
            above = D[r + 1 : r + 1 + n] * T[1, r + 1 : r + 1 + n]
            below = D[r - 1 : r - 1 + n] * T[1, r - 1 : r - 1 + n]
            T[2, r : r + n] = T[2, r : r + n] - (dlon(du) + (above - below))
        edge_rows(T, rows, keep_top, keep_bottom)
        for r, n in row_blocks(rows):
            f = F[r : r + n]
            v = T[1, r : r + n]
            u = T[0, r : r + n] + f * v - HALF * dlon(T[2, r : r + n])
            T[0, r : r + n] = u
            T[1, r : r + n] = v - f * u - HALF * (T[2, r + 1 : r + 1 + n] - T[2, r - 1 : r - 1 + n])
        return carry

    lax.fori_loop(0, STEPS, step, 0)


def adjoint(T, D, F, rows, keep_top, keep_bottom):
    def step(_, carry):
        for r, n in row_blocks(rows):
            a = T[0, r : r + n] - F[r : r + n] * T[1, r : r + n]
            T[0, r : r + n] = a
            T[2, r : r + n] = T[2, r : r + n] + HALF * (
                (T[1, r + 1 : r + 1 + n] - T[1, r - 1 : r - 1 + n]) + dlon(a)
            )
        edge_rows(T, rows, keep_top, keep_bottom)
        for r, n in row_blocks(rows):
            a = T[0, r : r + n]
            d = D[r : r + n]
            T[0, r : r + n] = a + d * dlon(T[2, r : r + n])
            T[1, r : r + n] = (
                T[1, r : r + n]
                + F[r : r + n] * a
                + d * (T[2, r + 1 : r + 1 + n] - T[2, r - 1 : r - 1 + n])
            )
        return carry

    lax.fori_loop(0, STEPS, step, 0)


def deposit_kernel(count, code_ref, w_ref, wy_ref, out_w, out_wy, *more):
    grids = [(out_w, out_wy)] + [(more[2 * i], more[2 * i + 1]) for i in range(STREAMS - 1)]
    total = out_w.shape[0]
    zero = jnp.zeros((64, 128), jnp.float32)

    def clear(i, carry):
        at = pl.ds(pl.multiple_of(i * 64, 64), 64)
        for gw, gy in grids:
            gw[at, :] = zero
            gy[at, :] = zero
        return carry

    lax.fori_loop(0, total // 64, clear, 0)
    lanes = lax.broadcasted_iota(jnp.int32, (1, 128), 1)

    def add(i, carry):
        for s, (gw, gy) in enumerate(grids):
            j = i * STREAMS + s
            code = code_ref[j]
            at = pl.ds(code // 128, 1)
            hit = lanes == code % 128
            gw[at, :] = gw[at, :] + jnp.where(hit, w_ref[j], 0.0)
            gy[at, :] = gy[at, :] + jnp.where(hit, wy_ref[j], 0.0)
        return carry

    lax.fori_loop(0, count // STREAMS, add, 0)

    def gather(i, carry):
        at = pl.ds(pl.multiple_of(i * 64, 64), 64)
        out_w[at, :] = sum([g[0][at, :] for g in grids[1:]], out_w[at, :])
        out_wy[at, :] = sum([g[1][at, :] for g in grids[1:]], out_wy[at, :])
        return carry

    lax.fori_loop(0, total // 64, gather, 0)


def place():
    tm, sp = lax.axis_index("tm"), lax.axis_index("space")
    a, y, b, c = tm % 2, tm // 2, sp // 2, sp % 2
    return tm, sp, a, y, b, c, 2 * b + a, 2 * y + c


def main_kernel(
    rows, cells, pairs, bands,
    x_own, x_got, e_hbm, d_hbm, s_hbm, w_hbm, wy_hbm, f_hbm, c0_ref,
    out_hbm, cost_ref,
    stg_x, stg_e, stg_d, stg_s, X, T, A, D, F, E, W, WY, XN, EN, FIN, OUT, cbuf, crecv,
    load_sem, push_send, push_recv, halo_send, halo_recv,
    x_send, x_recv, e_send, e_recv, fin_send, fin_recv, c_send, c_recv, out_sem,
):
    tm, sp, a, y, b, c, band, window = place()
    last = 2 * pairs - 1
    own = a == c
    partner = (tm, 2 * b + (1 - c))
    swap = (2 * y + (1 - a), 2 * b + (1 - c))
    up_band, down_band = lax.rem(band + bands - 1, bands), lax.rem(band + 1, bands)
    up = (2 * y + up_band % 2, 2 * (up_band // 2) + c)
    down = (2 * y + down_band % 2, 2 * (down_band // 2) + c)
    succ_y = lax.rem(y + c, pairs)
    succ = (2 * succ_y + a, 2 * b + (1 - c))
    pred_y = lax.rem(y + pairs - (1 - c), pairs)
    pred = (2 * pred_y + a, 2 * b + (1 - c))
    not_top, not_bottom = band > 0, band < bands - 1
    not_first, not_last = window > 0, window < last
    keep_top = jnp.where(not_top, 1.0, 0.0).astype(jnp.float32)
    keep_bottom = jnp.where(not_bottom, 1.0, 0.0).astype(jnp.float32)
    chunk = rows // len(ORDER)
    inner = pl.ds(TOP, rows)

    loads = [
        pltpu.make_async_copy(src, dst, load_sem.at[i])
        for i, (src, dst) in enumerate(((w_hbm, W), (wy_hbm, WY), (f_hbm, F)))
    ]
    for load in loads:
        load.start()
    load_own = pltpu.make_async_copy(x_own, stg_x, load_sem.at[3])
    load_got = pltpu.make_async_copy(x_got, stg_x, load_sem.at[3])
    load_e = pltpu.make_async_copy(e_hbm, stg_e, load_sem.at[4])
    load_d = pltpu.make_async_copy(d_hbm, stg_d, load_sem.at[5])
    load_s = pltpu.make_async_copy(s_hbm, stg_s, load_sem.at[6])

    @pl.when(own)
    def _():
        load_own.start()
        load_e.start()
        load_d.start()

    @pl.when(jnp.logical_not(own))
    def _():
        load_got.start()

    own_start = own & (y == 0) & (c == 0)
    push_start = own & (y == 0) & (c == 1)
    need_start = jnp.logical_not(own) & (y == 0) & (c == 0)

    @pl.when(own_start)
    def _():
        load_s.start()

    zeros = jnp.zeros((TOP, 8, 128), jnp.float32)
    for buf in (X, A):
        for i in range(3):
            buf[i, 0:TOP] = zeros
            buf[i, TOP + rows : 2 * TOP + rows] = zeros
    D[0:TOP] = zeros
    D[TOP + rows : 2 * TOP + rows] = zeros

    barrier = pltpu.get_barrier_semaphore()
    for da in range(2):
        for s in range(bands):
            other = jnp.logical_not((a == da) & (sp == s))

            @pl.when(other)
            def _(da=da, s=s):
                pl.semaphore_signal(barrier, inc=1, device_id=(2 * y + da, s), device_id_type=MESH)

    far = jnp.where(c == 1, not_last, not_first)
    far_y = jnp.where(c == 1, succ_y, pred_y)

    @pl.when(far)
    def _():
        pl.semaphore_signal(
            barrier, inc=1, device_id=(2 * far_y + a, 2 * b + (1 - c)), device_id_type=MESH
        )

    pl.semaphore_wait(barrier, 2 * bands - 1 + far.astype(jnp.int32))

    def remote(src, dst, send, recv, to):
        return pltpu.make_async_remote_copy(
            src_ref=src, dst_ref=dst, send_sem=send, recv_sem=recv, device_id=to, device_id_type=MESH
        )

    push_e = remote(e_hbm, stg_e, push_send.at[0], push_recv.at[0], partner)
    push_d = remote(d_hbm, stg_d, push_send.at[1], push_recv.at[1], partner)
    push_s = remote(s_hbm, stg_s, push_send.at[2], push_recv.at[2], partner)

    @pl.when(own)
    def _():
        push_d.start()
        push_e.start()

    @pl.when(push_start)
    def _():
        push_s.start()

    def to_rows(stage, store, count):
        def body(i, carry):
            for j in range(8):
                store(i * 8 + j, stage[pl.ds(i * 64 + j, 8, stride=8), :])
            return carry

        lax.fori_loop(0, count // 8, body, 0)

    def three(stage, buf, top):
        def body(i, carry):
            for comp in range(3):
                for j in range(8):
                    buf[comp, top + i * 8 + j] = stage[
                        pl.ds(comp * rows * 8 + i * 64 + j, 8, stride=8), :
                    ]
            return carry

        lax.fori_loop(0, rows // 8, body, 0)

    load_own.wait()
    three(stg_x, X, TOP)

    def chunk_copy(src, src_top, dst, dst_top, j, send, recv, to):
        return remote(
            src.at[:, pl.ds(src_top + j * chunk, chunk)],
            dst.at[:, pl.ds(dst_top + j * chunk, chunk)],
            send,
            recv,
            to,
        )

    def x_copy(it, j):
        return chunk_copy(X, TOP, XN.at[it], 0, j, x_send.at[it, j], x_recv.at[it, j], pred)

    def e_copy(it, j):
        return chunk_copy(T, TOP, EN.at[it], 0, j, e_send.at[it, j], e_recv.at[it, j], succ)

    def fin_copy(j):
        return chunk_copy(X, TOP, FIN, 0, j, fin_send.at[j], fin_recv.at[j], swap)

    def halo_copies(view, h):
        return (
            remote(
                view(TOP), view(TOP + rows), halo_send.at[h, 0], halo_recv.at[h, 0], up
            ),
            remote(
                view(TOP + rows - HALO), view(TOP - HALO), halo_send.at[h, 1], halo_recv.at[h, 1], down
            ),
        )

    def start_halo(view, h):
        to_up, to_down = halo_copies(view, h)

        @pl.when(not_top)
        def _():
            to_up.start()

        @pl.when(not_bottom)
        def _():
            to_down.start()

    def wait_halo(view, h):
        to_up, to_down = halo_copies(view, h)

        @pl.when(not_top)
        def _():
            to_up.wait_send()
            to_down.wait_recv()

        @pl.when(not_bottom)
        def _():
            to_down.wait_send()
            to_up.wait_recv()

    def view_x(r):
        return X.at[:, pl.ds(r, HALO)]

    def view_a(r):
        return A.at[:, pl.ds(r, HALO)]

    def view_d(r):
        return D.at[pl.ds(r, HALO)]

    @pl.when(not_first)
    def _():
        for j in ORDER:
            x_copy(0, j).start()

    start_halo(view_x, 0)

    @pl.when(own)
    def _():
        load_d.wait()

    @pl.when(jnp.logical_not(own))
    def _():
        push_d.wait_recv()

    def store_d(r, value):
        D[TOP + r] = HALF * value

    to_rows(stg_d, store_d, rows)
    start_halo(view_d, 4)

    @pl.when(own)
    def _():
        load_e.wait()
        push_d.wait_send()
        push_e.wait_send()

    @pl.when(jnp.logical_not(own))
    def _():
        push_e.wait_recv()

    three(stg_e, E, 0)

    @pl.when(own_start)
    def _():
        load_s.wait()

    @pl.when(push_start)
    def _():
        push_s.wait_send()

    @pl.when(need_start)
    def _():
        push_s.wait_recv()

    @pl.when(window == 0)
    def _():
        three(stg_s, EN.at[0], 0)
        three(stg_s, EN.at[1], 0)

    for load in loads:
        load.wait()
    wait_halo(view_d, 4)

    for it in range(ITERS):
        final = it == ITERS - 1
        wait_halo(view_x, it)

        def take(i, carry):
            for comp in range(3):
                at = pl.ds(TOP - HALO + i * 8, 8)
                T[comp, at] = X[comp, at]
            return carry

        lax.fori_loop(0, (rows + 2 * HALO) // 8, take, 0)
        forward(T, D, F, rows, keep_top, keep_bottom)

        @pl.when(not_last)
        def _():
            for j in ORDER:
                e_copy(it, j).start()

        for n, j in enumerate(ORDER):

            @pl.when(not_last)
            def _():
                x_copy(it, j).wait_recv()

            def differ(i, carry):
                at = pl.ds(j * chunk + i * 4, 4)
                wide = pl.ds(TOP + j * chunk + i * 4, 4)
                for comp in range(3):
                    value = E[comp, at] * (XN[it, comp, at] - T[comp, wide])
                    A[comp, wide] = jnp.where(not_last, value, 0.0)
                return carry

            lax.fori_loop(0, chunk // 4, differ, 0)
            if n == 1:
                start_halo(view_a, 2 + it)

        wait_halo(view_a, 2 + it)
        adjoint(A, D, F, rows, keep_top, keep_bottom)

        acc = 0.5 * c0_ref[...]
        for n, j in enumerate(ORDER):

            @pl.when(not_first)
            def _():
                x_copy(it, j).wait_send()
                e_copy(it, j).wait_recv()

            def update(i, acc):
                at = pl.ds(j * chunk + i * 4, 4)
                wide = pl.ds(TOP + j * chunk + i * 4, 4)
                for comp in range(3):
                    x = X[comp, wide]
                    gap = x - EN[it, comp, at]
                    lam = E[comp, at] * gap
                    wy = WY[comp, at]
                    grad = W[comp, at] * x - wy
                    acc = acc + 0.5 * jnp.sum(lam * gap + x * (grad - wy), axis=0)
                    X[comp, wide] = x - STEP_SIZE * (lam - A[comp, wide] + grad)
                return acc

            acc = lax.fori_loop(0, chunk // 4, update, acc)
            if final:

                @pl.when(jnp.logical_not(own))
                def _():
                    fin_copy(j).start()

            else:

                @pl.when(not_first)
                def _():
                    x_copy(it + 1, j).start()

                if n == 1:
                    start_halo(view_x, it + 1)

        cbuf[it] = acc

        @pl.when(not_last)
        def _():
            for j in ORDER:
                e_copy(it, j).wait_send()

    def c_copy(s):
        return remote(cbuf, crecv.at[band], c_send.at[s], c_recv.at[band], (2 * y + c, s))

    for s in range(bands):

        @pl.when(jnp.logical_not(own & (sp == s)))
        def _(s=s):
            c_copy(s).start()

    @pl.when(own)
    def _():
        crecv[band] = cbuf[...]

    def out_copy(comp, j):
        at = pl.ds((comp * rows + j * chunk) * 8, chunk * 8)
        return pltpu.make_async_copy(OUT.at[at], out_hbm.at[at], out_sem.at[comp, j])

    def put(src, top, j):
        def body(i, carry):
            for comp in range(3):
                for r in range(8):
                    at = pl.ds(comp * rows * 8 + j * chunk * 8 + i * 64 + r, 8, stride=8)
                    OUT[at, :] = src[comp, top + j * chunk + i * 8 + r]
            return carry

        lax.fori_loop(0, chunk // 8, body, 0)

    for j in ORDER:

        @pl.when(own)
        def _():
            put(X, TOP, j)

        @pl.when(jnp.logical_not(own))
        def _():
            fin_copy(j).wait_recv()
            put(FIN, 0, j)

        for comp in range(3):
            out_copy(comp, j).start()

    for s in range(bands):

        @pl.when(jnp.logical_not(own & (sp == s)))
        def _(s=s):
            c_copy(s).wait_send()

        @pl.when(jnp.logical_not(own & (band == s)))
        def _(s=s):
            remote(cbuf, crecv.at[s], c_send.at[s], c_recv.at[s], partner).wait_recv()

    total = crecv[0]
    for s in range(1, bands):
        total = total + crecv[s]
    for it in range(ITERS):
        cost_ref[it, 0] = jnp.sum(total[it]) / cells

    @pl.when(jnp.logical_not(own))
    def _():
        for j in ORDER:
            fin_copy(j).wait_send()

    for j in ORDER:
        for comp in range(3):
            out_copy(comp, j).wait()


def as_tiles(x):
    x = x.reshape(-1, 8, x.shape[-1] // 128, 128)
    return x.transpose(0, 2, 1, 3).reshape(-1, 128)


def from_tiles(x, shape):
    x = x.reshape(-1, shape[-1] // 128, 8, 128)
    return x.transpose(0, 2, 1, 3).reshape(shape)


def per_device(
    increments, start_state, depth, error_weight, obs_index, obs_count, obs_value, obs_weight
):
    rows, columns = increments.shape[2:]
    slots = obs_index.shape[1]
    bands, windows = lax.axis_size("space"), lax.axis_size("tm")
    pairs = windows // 2
    total_rows = rows * bands
    cells = 3 * total_rows * columns
    _, _, a, y, b, c, band, _ = place()
    own = a == c

    exchange = []
    for py in range(pairs):
        for pb in range(bands // 2):
            one = 2 * py * bands + 2 * pb + 1
            two = (2 * py + 1) * bands + 2 * pb
            exchange += [(one, two), (two, one)]
    both = ("tm", "space")

    live = jnp.arange(slots) < obs_count[0]
    packed = jnp.stack(
        [obs_index[0].astype(jnp.float32), jnp.where(live, obs_weight[0], 0.0), obs_value[0]]
    )
    packed_got = lax.ppermute(packed, both, exchange)
    x_got = lax.ppermute(increments, both, exchange)
    packed = jnp.where(own, packed, packed_got)

    index = packed[0].astype(jnp.int32)
    component = index // (total_rows * columns)
    line = index // columns % total_rows - band * rows
    inside = (line >= 0) & (line < rows)
    code = (component * rows + jnp.clip(line, 0, rows - 1)) * columns + index % columns
    weight = jnp.where(inside, packed[1], 0.0)
    weighted = weight * packed[2]
    c0 = jnp.sum((weighted * packed[2]).reshape(-1, 8, 128), 0)

    lines = 3 * rows * 8
    smem = pl.BlockSpec(memory_space=pltpu.SMEM)
    vmem = pl.BlockSpec(memory_space=pltpu.VMEM)
    hbm = pl.BlockSpec(memory_space=pl.ANY)
    grid_type = jax.ShapeDtypeStruct((lines, 128), jnp.float32)
    grid_w, grid_wy = pl.pallas_call(
        functools.partial(deposit_kernel, slots),
        out_shape=(grid_type, grid_type),
        in_specs=[smem] * 3,
        out_specs=(vmem, vmem),
        scratch_shapes=[pltpu.VMEM((lines, 128), jnp.float32)] * (2 * STREAMS - 2),
        cost_estimate=pl.CostEstimate(flops=10**7, bytes_accessed=4 * 10**7, transcendentals=0),
        name="deposit",
    )(code, weight, weighted)

    wide = rows + 2 * TOP
    latitude = ((band * rows - TOP + jnp.arange(wide)).astype(jnp.float32) + 0.5) / total_rows
    rate = CORIOLIS_MAX * jnp.sin(latitude * math.pi - math.pi / 2)
    rate = jnp.broadcast_to(rate[:, None, None], (wide, 8, 128))

    def rows_of(count, lead=(3,)):
        return pltpu.VMEM((*lead, count, 8, 128), jnp.float32)

    tiles = pltpu.VMEM((lines, 128), jnp.float32)
    dma = pltpu.SemaphoreType.DMA
    chunks = len(ORDER)
    out, costs = pl.pallas_call(
        functools.partial(main_kernel, rows, cells, pairs, bands),
        out_shape=(grid_type, jax.ShapeDtypeStruct((ITERS, 1), jnp.float32)),
        in_specs=[hbm] * 8 + [vmem],
        out_specs=(hbm, smem),
        scratch_shapes=[
            tiles, tiles, pltpu.VMEM((rows * 8, 128), jnp.float32), tiles,
            rows_of(wide), rows_of(wide), rows_of(wide),
            rows_of(wide, ()), rows_of(wide, ()),
            rows_of(rows), rows_of(rows), rows_of(rows),
            rows_of(rows, (ITERS, 3)), rows_of(rows, (ITERS, 3)), rows_of(rows), tiles,
            pltpu.VMEM((ITERS, 8, 128), jnp.float32), pltpu.VMEM((bands, ITERS, 8, 128), jnp.float32),
            dma((7,)), dma((3,)), dma((3,)), dma((5, 2)), dma((5, 2)),
            dma((ITERS, chunks)), dma((ITERS, chunks)), dma((ITERS, chunks)), dma((ITERS, chunks)),
            dma((chunks,)), dma((chunks,)), dma((bands,)), dma((bands,)), dma((3, chunks)),
        ],
        compiler_params=pltpu.CompilerParams(
            collective_id=0, has_side_effects=True, vmem_limit_bytes=56 * 2**20
        ),
        name="iterations",
    )(
        as_tiles(increments), as_tiles(x_got), as_tiles(error_weight), as_tiles(depth),
        as_tiles(start_state), grid_w.reshape(3, rows, 8, 128), grid_wy.reshape(3, rows, 8, 128),
        rate, c0,
    )
    return from_tiles(out, increments.shape), costs


def solution(mesh):
    placed = (
        P("tm", None, "space", None),
        P(None, "space", None),
        P("space", None),
        P(None, "space", None),
        P("tm", None),
        P("tm"),
        P("tm", None),
        P("tm", None),
    )
    return jax.shard_map(
        per_device,
        mesh=mesh,
        in_specs=placed,
        out_specs=(P("tm", None, "space", None), P(None, "tm")),
        check_vma=False,
    )
```

profile of v0, /device:TPU:129, one launch (start us, length us, event | category | flops | bytes accessed | tf_op | source)
XLA Modules:
  0.0 126.2 jit_solution(6199972144707624720)
XLA Ops:
  1.3 0.7 convert_element_type.25
  2.0 0.7 compare_select_fusion
  2.8 0.8 pad_maximum_fusion
  3.5 3.7 %collective-permute-start.1 = (f32[3,4096]{1,0:T(4,128)S(1)}, f32[3,4096]{1,0:T(4,128)S(1)}, u32[]{:S(2)}, u32[]{:S(2)}) collective-permute-start(f32[3,4096]{1,0:T(4,128)S(1)} %pad_maximum_fusion), channel_id=1, source_target_pairs={{1,4},{4,1},{3,6},{6,3},{9,12},{12,9},{11,14},{14,11},{17,20},{20,... | collective-permute-start | bytes 147464 | tf_op jit(solution)/shard_map/ppermute | solution.py:552
  7.2 1.9 %collective-permute-start = (f32[1,3,128,1024]{3,2,1,0:T(8,128)}, f32[1,3,128,1024]{3,2,1,0:T(8,128)S(1)}, u32[]{:S(2)}, u32[]{:S(2)}) collective-permute-start(f32[1,3,128,1024]{3,2,1,0:T(8,128)} %param.8), channel_id=1, source_target_pairs={{1,4},{4,1},{3,6},{6,3},{9,12},{12,9},{11,14},{14,11},{17,20},{20,... | collective-permute-start | bytes 4718600 | tf_op jit(solution)/shard_map/ppermute | solution.py:553
  9.2 0.0 collective-permute-done.1
  9.2 0.8 broadcast_select_fusion
  10.1 0.6 fusion.4.code_ref
  10.7 0.6 fusion.14
  11.3 37.2 %deposit.1 = (f32[3072,128]{1,0:T(8,128)}, f32[3072,128]{1,0:T(8,128)}) custom-call(s32[4096]{0:T(1024)} %fusion.4.code_ref, f32[4096]{0:T(1024)} %get-tuple-element.13.w_ref, f32[4096]{0:T(1024)} %get-tuple-element.12.wy_ref), custom_call_target="tpu_custom_call" | custom-call | flops 10000000 | bytes 40000000 | tf_op jit(solution)/shard_map/deposit/pallas_call | solution.py:570
  48.5 0.6 fusion.10.c0_ref
  49.1 0.0 collective-permute-done
  49.1 0.0 copy-start
  49.1 1.3 %broadcast_in_dim.17.f_hbm = f32[160,8,128]{2,1,0:T(8,128)} broadcast(f32[160]{0:T(256)S(1)} %sine_multiply_fusion), dimensions={0} | broadcast | bytes 656000 | tf_op jit(solution)/shard_map/broadcast_in_dim | solution.py:583
  50.4 0.1 copy-done
  50.5 71.8 %iterations.1 = (f32[3072,128]{1,0:T(8,128)}, f32[2,1]{1,0:T(2,128)}) custom-call(f32[3072,128]{1,0:T(8,128)} %bitcast.40, f32[3072,128]{1,0:T(8,128)} %bitcast.43, f32[3072,128]{1,0:T(8,128)} %bitcast.41, f32[1024,128]{1,0:T(8,128)} %bitcast.47, f32[3072,128]{1,0:T(8,128)} %bitcast.42, f32[3,128,8,128]{3,2,1,0:T(8,128)} %bitcast.44, ...), custom_call_target="tpu_custom_call" | custom-call | tf_op jit(solution)/shard_map/iterations/pallas_call | solution.py:591
  122.3 1.2 copy.10
  123.5 2.7 %copy.13 = f32[1,3,128,1024]{3,2,1,0:T(8,128)} copy(f32[1,3,128,1024]{3,2,1,0:T(8,128)} %bitcast.46) | data formatting | bytes 3145728
  (2 shorter events, 0.1 us)
Async XLA Ops:
  3.5 5.7 %collective-permute-start.1 = (f32[3,4096]{1,0:T(4,128)S(1)}, f32[3,4096]{1,0:T(4,128)S(1)}, u32[]{:S(2)}, u32[]{:S(2)}) collective-permute-start(f32[3,4096]{1,0:T(4,128)S(1)} %pad_maximum_fusion), channel_id=1, source_target_pairs={{1,4},{4,1},{3,6},{6,3},{9,12},{12,9},{11,14},{14,11},{17,20},{20,... | collective-permute-start | bytes 147464 | tf_op jit(solution)/shard_map/ppermute | solution.py:552
  7.2 41.9 %collective-permute-start = (f32[1,3,128,1024]{3,2,1,0:T(8,128)}, f32[1,3,128,1024]{3,2,1,0:T(8,128)S(1)}, u32[]{:S(2)}, u32[]{:S(2)}) collective-permute-start(f32[1,3,128,1024]{3,2,1,0:T(8,128)} %param.8), channel_id=1, source_target_pairs={{1,4},{4,1},{3,6},{6,3},{9,12},{12,9},{11,14},{14,11},{17,20},{20,... | collective-permute-start | bytes 4718600 | tf_op jit(solution)/shard_map/ppermute | solution.py:553
  49.1 1.4 %copy-start = (f32[1,3,128,1024]{3,2,1,0:T(8,128)}, f32[1,3,128,1024]{3,2,1,0:T(8,128)S(1)}, u32[]{:S(2)}) copy-start(f32[1,3,128,1024]{3,2,1,0:T(8,128)S(1)} %collective-permute-done) | copy-start | bytes 4718596
where the time goes:
time: 127 us; the launch traced here: 126 us
  Pallas kernels  109 us (86%)
  starting transfers between devices  5.6 us (4%)
  local copies, waits for them, and re-layouts  5.3 us (4%)
  other arithmetic  5 us (4%)
  between operations  1.37 us (1%)
    pallas_call x1, Pallas kernels, per_device(): pl.pallas_call(functools.partial(main_kernel, rows, cells, pairs, bands),...  71.8 us
    pallas_call x1, Pallas kernels, per_device(): pl.pallas_call(functools.partial(deposit_kernel, slots), out_shape=(grid_...  37.2 us
    unnamed x4, local copies, waits for them, and re-layouts  4.03 us
    ppermute x1, starting transfers between devices, per_device(): packed_got = lax.ppermute(packed, both, exchange)  3.68 us
  transfers between devices with their start and end apart: 2, of which 0 were waited for; matrix products, arithmetic and copies ran while one was open for 2% of the time, Pallas kernels for 29%

commit v1 on v0

v1 whole, which is shorter than its diff:
```python
import functools
import math

import jax
import jax.numpy as jnp
from jax import lax
from jax.experimental import pallas as pl
from jax.experimental.pallas import tpu as pltpu
from jax.sharding import PartitionSpec as P

STEPS = 6
ITERS = 2
COURANT = 0.35
HALF = 0.5 * COURANT
CORIOLIS_MAX = 0.2
STEP_SIZE = 0.2
HALO = 2 * STEPS
TOP = 24
BLK = 8
STREAMS = 2
UNROLL = 16
VMEM = 36
SCHEDULE = (
    "A00", "U00", "A01", "U01", "A02", "U02", "F10", "E10", "F11",
    "A03", "U03", "F12", "F13", "A10", "U10", "A11", "U11", "A12",
    "U12", "F14", "E11", "A13", "U13", "A14", "U14",
)
MESH = pl.DeviceIdType.MESH


def dlon(f):
    lane = lax.broadcasted_iota(jnp.int32, f.shape, 2)
    g = pltpu.roll(f, 127, axis=2)
    g = jnp.where(lane == 127, pltpu.roll(g, 7, axis=1), g)
    m = pltpu.roll(f, 1, axis=2)
    m = jnp.where(lane == 0, pltpu.roll(m, 1, axis=1), m)
    return g - m


def slab(T, low, high, first, second, edge):
    for s in range(STEPS):
        for r in range(low, high, BLK):
            first(r - 1 - 2 * s, min(BLK, high - r))
        if edge is not None:
            T[2, TOP - 1] = T[2, TOP - 1] * edge
        for r in range(low, high, BLK):
            second(r - 2 - 2 * s, min(BLK, high - r))


def forward(T, D, F, low, high, edge):
    def first(r, n):
        at = pl.ds(r, n)
        above, below = pl.ds(r + 1, n), pl.ds(r - 1, n)
        du = D[at] * T[0, at]
        T[2, at] = T[2, at] - (dlon(du) + (D[above] * T[1, above] - D[below] * T[1, below]))

    def second(r, n):
        at = pl.ds(r, n)
        f = F[at]
        v = T[1, at]
        u = T[0, at] + f * v - HALF * dlon(T[2, at])
        T[0, at] = u
        T[1, at] = v - f * u - HALF * (T[2, pl.ds(r + 1, n)] - T[2, pl.ds(r - 1, n)])

    slab(T, low, high, first, second, edge)


def adjoint(T, D, F, low, high, edge):
    def first(r, n):
        at = pl.ds(r, n)
        a = T[0, at] - F[at] * T[1, at]
        T[0, at] = a
        T[2, at] = T[2, at] + HALF * ((T[1, pl.ds(r + 1, n)] - T[1, pl.ds(r - 1, n)]) + dlon(a))

    def second(r, n):
        at = pl.ds(r, n)
        a = T[0, at]
        d = D[at]
        T[0, at] = a + d * dlon(T[2, at])
        T[1, at] = T[1, at] + F[at] * a + d * (T[2, pl.ds(r + 1, n)] - T[2, pl.ds(r - 1, n)])

    slab(T, low, high, first, second, edge)


def deposit_kernel(count, code_ref, w_ref, wy_ref, out_w, out_wy, *more):
    grids = [(out_w, out_wy)] + [(more[2 * i], more[2 * i + 1]) for i in range(STREAMS - 1)]
    total = out_w.shape[0]
    zero = jnp.zeros((64, 128), jnp.float32)

    def clear(i, carry):
        at = pl.ds(pl.multiple_of(i * 64, 64), 64)
        for gw, gy in grids:
            gw[at, :] = zero
            gy[at, :] = zero
        return carry

    lax.fori_loop(0, total // 64, clear, 0)
    lanes = lax.broadcasted_iota(jnp.int32, (1, 128), 1)

    def add(i, carry):
        for k in range(UNROLL):
            for s, (gw, gy) in enumerate(grids):
                j = (i * UNROLL + k) * STREAMS + s
                code = code_ref[j]
                at = pl.ds(lax.shift_right_logical(code, 7), 1)
                hit = lanes == (code & 127)
                gw[at, :] = gw[at, :] + jnp.where(hit, w_ref[j], 0.0)
                gy[at, :] = gy[at, :] + jnp.where(hit, wy_ref[j], 0.0)
        return carry

    lax.fori_loop(0, count // (STREAMS * UNROLL), add, 0)

    def gather(i, carry):
        at = pl.ds(pl.multiple_of(i * 64, 64), 64)
        out_w[at, :] = sum([g[0][at, :] for g in grids[1:]], out_w[at, :])
        out_wy[at, :] = sum([g[1][at, :] for g in grids[1:]], out_wy[at, :])
        return carry

    lax.fori_loop(0, total // 64, gather, 0)


def place():
    tm, sp = lax.axis_index("tm"), lax.axis_index("space")
    a, y, b, c = tm % 2, tm // 2, sp // 2, sp % 2
    return tm, sp, a, y, b, c, 2 * b + a, 2 * y + c


def limits(rows):
    forward_high = [rows * 3 // 8, rows * 5 // 8, rows * 7 // 8, rows + HALO]
    plan = []
    for _ in range(ITERS):
        e = [r - HALO for r in forward_high]
        adjoint_high = e[:-1] + [rows + HALO]
        u = [r - HALO for r in adjoint_high]
        plan.append((forward_high, e, adjoint_high, u))
        forward_high = u + [rows + HALO]
    return plan


def sent_pieces(rows):
    edge = rows - HALO
    plan = limits(rows)
    x, later = plan[0][0], plan[0][3]
    first = [(0, HALO), (edge, rows), (HALO, x[0])] + list(zip(x[:-2], x[1:-1])) + [(x[-2], edge)]
    then = list(zip([0] + later[:-2], later[:-1])) + [(edge, rows), (later[-2], edge)]
    return first, then


def main_kernel(
    rows, cells, pairs, bands,
    x_own, x_got, e_own, d_own, s_own, W, WY, F, c0_ref,
    OUT, cost_ref,
    stg_e, stg_d, stg_s, X, T, A, D, E, XN, EN, FIN, cbuf, crecv,
    edge_out, edge_in, d_top, d_bottom,
    push_send, push_recv, halo_send, halo_recv,
    x_send, x_recv, e_send, e_recv, fin_send, fin_recv, c_send, c_recv,
):
    tm, sp, a, y, b, c, band, window = place()
    last = 2 * pairs - 1
    own = a == c
    partner = (tm, 2 * b + (1 - c))
    swap = (2 * y + (1 - a), 2 * b + (1 - c))
    flip = a == 1
    sign = jnp.where(flip, -1.0, 1.0).astype(jnp.float32)
    bottom_peer = (2 * y + (1 - a), sp)
    top_band = jnp.where(flip, band + 1, band - 1)
    has_top = (top_band >= 0) & (top_band < bands)
    top_band = lax.rem(top_band + bands, bands)
    top_peer = (2 * y + top_band % 2, 2 * (top_band // 2) + c)
    succ_y = lax.rem(y + c, pairs)
    succ = (2 * succ_y + a, 2 * b + (1 - c))
    pred_y = lax.rem(y + pairs - (1 - c), pairs)
    pred = (2 * pred_y + a, 2 * b + (1 - c))
    not_first, not_last = window > 0, window < last
    edge = jnp.where(has_top, 1.0, 0.0).astype(jnp.float32)
    plan = limits(rows)
    pieces = sent_pieces(rows)

    edge_lines = pl.ds(pl.multiple_of(jnp.where(flip, rows * 8 - 128, 0), 128), 128)
    own_start = own & (y == 0) & (c == 0)
    push_start = own & (y == 0) & (c == 1)
    need_start = jnp.logical_not(own) & (y == 0) & (c == 0)

    barrier = pltpu.get_barrier_semaphore()
    for da in range(2):
        for s in range(bands):
            other = jnp.logical_not((a == da) & (sp == s))

            @pl.when(other)
            def _(da=da, s=s):
                pl.semaphore_signal(barrier, inc=1, device_id=(2 * y + da, s), device_id_type=MESH)

    far = jnp.where(c == 1, not_last, not_first)
    far_y = jnp.where(c == 1, succ_y, pred_y)

    @pl.when(far)
    def _():
        pl.semaphore_signal(
            barrier, inc=1, device_id=(2 * far_y + a, 2 * b + (1 - c)), device_id_type=MESH
        )

    zeros = jnp.zeros((TOP, 8, 128), jnp.float32)
    D[0:TOP] = zeros
    for it in range(ITERS):
        for i in range(3):
            T[it, i, 0:TOP] = zeros
            A[it, i, 0:TOP] = zeros

    def blocks(low, high, size, body, init=0):
        return lax.fori_loop(
            0, (high - low) // size, lambda i, carry: body(low + i * size, carry), init
        )

    def line_of(comp, r, j):
        line = jnp.where(flip, (rows - 8 - r) * 8 + 7 - j, r * 8 + j)
        return pl.ds(comp * rows * 8 + line, 8, stride=8)

    def each_row(stage, comps, store):
        def body(r, carry):
            for comp in range(comps):
                for j in range(8):
                    store(comp, r + j, stage[line_of(comp, r, j), :])
            return carry

        blocks(0, rows, 8, body)

    def store_x(comp, r, value):
        if comp == 1:
            value = value * sign
        X[comp, r] = value
        T[0, comp, TOP + r] = value

    @pl.when(own)
    def _():
        each_row(x_own, 3, store_x)

    @pl.when(jnp.logical_not(own))
    def _():
        each_row(x_got, 3, store_x)

    pl.semaphore_wait(barrier, 2 * bands - 1 + far.astype(jnp.int32))

    def remote(src, dst, send, recv, to):
        return pltpu.make_async_remote_copy(
            src_ref=src, dst_ref=dst, send_sem=send, recv_sem=recv, device_id=to, device_id_type=MESH
        )

    push_e = remote(e_own, stg_e, push_send.at[0], push_recv.at[0], partner)
    push_d = remote(d_own, stg_d, push_send.at[1], push_recv.at[1], partner)
    push_s = remote(s_own, stg_s, push_send.at[2], push_recv.at[2], partner)

    push_bottom = remote(d_own.at[edge_lines], d_bottom, push_send.at[3], push_recv.at[3], partner)
    push_top = [
        remote(
            d_own.at[edge_lines], d_top, push_send.at[4 + i], push_recv.at[4], (top_peer[0], 2 * (top_band // 2) + i)
        )
        for i in range(2)
    ]

    @pl.when(own)
    def _():
        push_d.start()
        pl.when(has_top)(lambda: [push.start() for push in push_top] and None)

    @pl.when(jnp.logical_not(own))
    def _():
        push_bottom.start()

    @pl.when(push_start)
    def _():
        push_s.start()

    def piece(ref, low, high, top):
        return ref.at[:, pl.ds(top + low, high - low)]

    def span(ends, j):
        return (ends[j - 1] if j else 0), ends[j]

    def x_copy(it, i):
        low, high = pieces[it][i]
        return remote(
            piece(X, low, high, 0), piece(XN.at[it], low, high, 0), x_send.at[it, i], x_recv.at[it, i], pred
        )

    arrived, sent, late = set(), set(), {}

    def some(done, it, low, high):
        fresh = [i for i, (p, q) in enumerate(pieces[it]) if p < high and q > low and (it, i) not in done]
        done.update((it, i) for i in fresh)
        return fresh

    def need_x(it, low, high):
        fresh = some(arrived, it, low, high)

        @pl.when(not_last)
        def _():
            for i in fresh:
                x_copy(it, i).wait_recv()

    def need_sent(it, low, high):
        fresh = some(sent, it, low, high)

        @pl.when(not_first)
        def _():
            for i in fresh:
                x_copy(it, i).wait_send()

    def send_x(it, low, high):
        @pl.when(not_first)
        def _():
            for i, (p, q) in enumerate(pieces[it]):
                if p >= low and q <= high:
                    x_copy(it, i).start()

    def e_copy(it, j):
        low, high = span(plan[it][1], j)
        return remote(
            piece(T.at[it], low, high, TOP), piece(EN.at[it], low, high, 0),
            e_send.at[it, j], e_recv.at[it, j], succ,
        )

    def fin_copy(j):
        low, high = span(plan[-1][3], j)
        return remote(piece(X, low, high, 0), piece(FIN, low, high, 0), fin_send.at[j], fin_recv.at[j], swap)

    def halo_copy(h, side):
        return remote(
            edge_out.at[h, side], edge_in.at[h, side], halo_send.at[h, side], halo_recv.at[h, side],
            bottom_peer if side else top_peer,
        )

    def send_halo(h, side, get):
        def pack():
            for comp in range(3):
                for i in range(HALO):
                    value = get(comp, rows - 1 - i if side else i)
                    edge_out[h, side, comp, i if side else HALO - 1 - i] = -value if comp == 1 else value
            halo_copy(h, side).start()

        if side:
            pack()
        else:
            pl.when(has_top)(pack)

    def take_halo(h, side, buf):
        def unpack():
            halo_copy(h, side).wait()
            at = TOP + rows if side else TOP - HALO
            for comp in range(3):
                buf[comp, at : at + HALO] = edge_in[h, side, comp]

        if side:
            unpack()
        else:
            pl.when(has_top)(unpack)

    send_x(0, 0, rows)
    for side in range(2):
        send_halo(0, side, lambda comp, r: X[comp, r])

    @pl.when(own)
    def _():
        push_e.start()

    def store_d(comp, r, value):
        D[TOP + r] = HALF * value

    @pl.when(own)
    def _():
        each_row(d_own, 1, store_d)

    @pl.when(jnp.logical_not(own))
    def _():
        push_d.wait_recv()
        each_row(stg_d, 1, store_d)


    def edge_line(i, mirrored, line=0):
        plain, back = i // 8 * 64 + i % 8, (15 - i) // 8 * 64 + (15 - i) % 8
        return pl.ds(line + jnp.where(mirrored, back, plain), 8, stride=8)

    def take_bottom(ref, line):
        for i in range(HALO):
            D[TOP + rows + i] = HALF * ref[edge_line(i, flip, line), :]

    @pl.when(own)
    def _():
        push_bottom.wait_recv()
        take_bottom(d_bottom, 0)

    @pl.when(jnp.logical_not(own))
    def _():
        take_bottom(d_own, jnp.where(flip, rows * 8 - 128, 0))

    @pl.when(has_top)
    def _():
        push_top[0].wait_recv()
        for i in range(HALO):
            D[TOP - 1 - i] = HALF * d_top[edge_line(i, jnp.logical_not(flip)), :]

    def run_forward(it, j):
        ends = plan[it][0]
        n = len(ends)
        if j == 0:
            take_halo(2 * it, 0, T.at[it])
        if j == n - 1:
            take_halo(2 * it, 1, T.at[it])
        low = TOP + ends[j - 1] if j else TOP - HALO + 2
        forward(T.at[it], D, F, low, TOP + ends[j], None if j else edge)
        pl.when(not_last)(lambda: e_copy(it, j).start())

    def send_edge(it, side):
        if side:
            need_x(it, rows - HALO, rows)
        else:
            early = some(arrived, it, 0, HALO)
            pl.when(not_last & has_top)(lambda: [x_copy(it, i).wait_recv() for i in early] and None)
            late[it] = early

        def get(comp, r):
            value = E[comp, r] * (XN[it, comp, r] - T[it, comp, TOP + r])
            return jnp.where(not_last, value, 0.0)

        send_halo(2 * it + 1, side, get)

    def run_adjoint(it, j):
        ends = plan[it][1]
        n = len(ends)
        low, high = span(ends, j)
        need_x(it, low, high)
        if j == 0:
            top_free = jnp.logical_not(has_top)
            pl.when(not_last & top_free)(lambda: [x_copy(it, i).wait_recv() for i in late[it]] and None)

        def differ(r, carry):
            at, wide = pl.ds(r, 4), pl.ds(TOP + r, 4)
            for comp in range(3):
                value = E[comp, at] * (XN[it, comp, at] - T[it, comp, wide])
                A[it, comp, wide] = jnp.where(not_last, value, 0.0)
            return carry

        blocks(low, high, 4, differ)
        if j == 0:
            take_halo(2 * it + 1, 0, A.at[it])
        if j == n - 1:
            take_halo(2 * it + 1, 1, A.at[it])
        low = TOP + low if j else TOP - HALO + 2
        adjoint(A.at[it], D, F, low, TOP + plan[it][2][j], None if j else edge)

    def run_update(it, j, acc):
        ends = plan[it][3]
        n = len(ends)
        final = it == ITERS - 1
        low, high = span(ends, j)

        @pl.when(not_first)
        def _():
            e_copy(it, j).wait_recv()

        need_sent(it, low, high)

        def update(r, acc):
            at, wide = pl.ds(r, 4), pl.ds(TOP + r, 4)
            for comp in range(3):
                x = X[comp, at]
                gap = x - EN[it, comp, at]
                lam = E[comp, at] * gap
                wy = WY[comp, at]
                grad = W[comp, at] * x - wy
                acc = acc + 0.5 * jnp.sum(lam * gap + x * (grad - wy), axis=0)
                x = x - STEP_SIZE * (lam - A[it, comp, wide] + grad)
                X[comp, at] = x
                if not final:
                    T[it + 1, comp, wide] = x
            return acc

        if high > low:
            acc = blocks(low, high, 4, update, acc)
            if final:
                pl.when(jnp.logical_not(own))(lambda: fin_copy(j).start())
            else:
                send_x(it + 1, low, high)
        if not final and j == 0:
            send_halo(2 * it + 2, 0, lambda comp, r: X[comp, r])
        if not final and j == n - 1:
            send_halo(2 * it + 2, 1, lambda comp, r: X[comp, r])
        return acc

    for j in range(len(plan[0][0])):
        run_forward(0, j)

    @pl.when(own)
    def _():
        push_d.wait_send()
        push_e.wait_send()
        pl.when(has_top)(lambda: [push.wait_send() for push in push_top] and None)

    @pl.when(jnp.logical_not(own))
    def _():
        push_e.wait_recv()
        push_bottom.wait_send()

    def store_e(comp, r, value):
        E[comp, r] = value

    pl.when(own)(lambda: each_row(e_own, 3, store_e))
    pl.when(jnp.logical_not(own))(lambda: each_row(stg_e, 3, store_e))

    pl.when(push_start)(lambda: push_s.wait_send())
    pl.when(need_start)(lambda: push_s.wait_recv())

    def store_s(comp, r, value):
        if comp == 1:
            value = value * sign
        EN[0, comp, r] = value
        EN[1, comp, r] = value

    pl.when(own_start)(lambda: each_row(s_own, 3, store_s))
    pl.when(need_start)(lambda: each_row(stg_s, 3, store_s))

    acc = [0.5 * c0_ref[...] for _ in range(ITERS)]
    send_edge(0, 0)
    send_edge(0, 1)
    for token in SCHEDULE:
        kind, it, j = token[0], int(token[1]), int(token[2])
        if kind == "F":
            run_forward(it, j)
        elif kind == "E":
            send_edge(it, j)
        elif kind == "A":
            run_adjoint(it, j)
        else:
            acc[it] = run_update(it, j, acc[it])
    for it in range(ITERS):
        cbuf[it] = acc[it]

    def c_copy(s):
        return remote(cbuf, crecv.at[band], c_send.at[s], c_recv.at[band], (2 * y + c, s))

    for s in range(bands):

        @pl.when(jnp.logical_not(own & (sp == s)))
        def _(s=s):
            c_copy(s).start()

    @pl.when(own)
    def _():
        crecv[band] = cbuf[...]

    flip_out = c == 1

    sign_out = jnp.where(flip_out, -1.0, 1.0).astype(jnp.float32)

    def put(src, j):
        low, high = span(plan[-1][3], j)

        def body(r, carry):
            for comp in range(3):
                for i in range(8):
                    value = src[comp, r + i]
                    line = jnp.where(flip_out, (rows - 8 - r) * 8 + 7 - i, r * 8 + i)
                    at = pl.ds(comp * rows * 8 + line, 8, stride=8)
                    OUT[at, :] = value * sign_out if comp == 1 else value
            return carry

        blocks(low, high, 8, body)

    used = [j for j in range(len(plan[-1][3])) if span(plan[-1][3], j)[1] > span(plan[-1][3], j)[0]]
    for j in used:

        @pl.when(own)
        def _():
            put(X, j)

        @pl.when(jnp.logical_not(own))
        def _():
            fin_copy(j).wait_recv()
            put(FIN, j)

    for s in range(bands):

        @pl.when(jnp.logical_not(own & (sp == s)))
        def _(s=s):
            c_copy(s).wait_send()

        @pl.when(jnp.logical_not(own & (band == s)))
        def _(s=s):
            remote(cbuf, crecv.at[s], c_send.at[s], c_recv.at[s], partner).wait_recv()

    total = crecv[0]
    for s in range(1, bands):
        total = total + crecv[s]
    for it in range(ITERS):
        cost_ref[0, it] = jnp.sum(total[it]) / cells

    @pl.when(not_last)
    def _():
        for it in range(ITERS):
            for j in range(len(plan[it][1])):
                e_copy(it, j).wait_send()

    @pl.when(jnp.logical_not(own))
    def _():
        for j in used:
            fin_copy(j).wait_send()


def as_tiles(x):
    x = x.reshape(-1, 8, x.shape[-1] // 128, 128)
    return x.transpose(0, 2, 1, 3).reshape(-1, 128)


def from_tiles(x, shape):
    x = x.reshape(-1, shape[-1] // 128, 8, 128)
    return x.transpose(0, 2, 1, 3).reshape(shape)


def per_device(
    increments, start_state, depth, error_weight, obs_index, obs_count, obs_value, obs_weight
):
    rows, columns = increments.shape[2:]
    slots = obs_index.shape[1]
    bands, windows = lax.axis_size("space"), lax.axis_size("tm")
    pairs = windows // 2
    total_rows = rows * bands
    cells = 3 * total_rows * columns
    _, _, a, y, b, c, band, _ = place()
    own = a == c

    exchange = []
    for py in range(pairs):
        for pb in range(bands // 2):
            one = 2 * py * bands + 2 * pb + 1
            two = (2 * py + 1) * bands + 2 * pb
            exchange += [(one, two), (two, one)]
    both = ("tm", "space")

    live = jnp.arange(slots) < obs_count[0]
    packed = jnp.stack(
        [obs_index[0].astype(jnp.float32), jnp.where(live, obs_weight[0], 0.0), obs_value[0]]
    )
    packed = lax.optimization_barrier(packed)
    packed_got = lax.ppermute(packed, both, exchange)
    x_got = lax.ppermute(increments, both, exchange)
    packed = jnp.where(own, packed, packed_got)

    index = packed[0].astype(jnp.int32)
    component = index // (total_rows * columns)
    line = index // columns % total_rows - band * rows
    inside = (line >= 0) & (line < rows)
    flip = a == 1
    line = jnp.where(flip, rows - 1 - line, line)
    code = (component * rows + jnp.clip(line, 0, rows - 1)) * columns + index % columns
    weight = jnp.where(inside, packed[1], 0.0)
    weighted = weight * packed[2]
    c0 = jnp.sum((weighted * packed[2]).reshape(-1, 8, 128), 0)
    weighted = jnp.where(flip & (component == 1), -weighted, weighted)

    wide = rows + 2 * TOP
    line = jnp.arange(wide) - TOP
    line = band * rows + jnp.where(flip, rows - 1 - line, line)
    latitude = (line.astype(jnp.float32) + 0.5) / total_rows
    rate = CORIOLIS_MAX * jnp.sin(latitude * math.pi - math.pi / 2)
    rate = jnp.where(flip, -rate, rate)
    rate = jnp.broadcast_to(rate[:, None, None], (wide, 8, 128))
    code, weight, weighted, rate, c0 = lax.optimization_barrier((code, weight, weighted, rate, c0))

    lines = 3 * rows * 8
    smem = pl.BlockSpec(memory_space=pltpu.SMEM)
    vmem = pl.BlockSpec(memory_space=pltpu.VMEM)
    grid_type = jax.ShapeDtypeStruct((lines, 128), jnp.float32)
    grid_w, grid_wy = pl.pallas_call(
        functools.partial(deposit_kernel, slots),
        out_shape=(grid_type, grid_type),
        in_specs=[smem] * 3,
        out_specs=(vmem, vmem),
        scratch_shapes=[pltpu.VMEM((lines, 128), jnp.float32)] * (2 * STREAMS - 2),
        compiler_params=pltpu.CompilerParams(vmem_limit_bytes=16 * 2**20),
        cost_estimate=pl.CostEstimate(flops=10**10, bytes_accessed=10**8, transcendentals=0),
        name="deposit",
    )(code, weight, weighted)

    def rows_of(count, lead=(3,)):
        return pltpu.VMEM((*lead, count, 8, 128), jnp.float32)

    tiles = pltpu.VMEM((lines, 128), jnp.float32)
    dma = pltpu.SemaphoreType.DMA
    chunks = len(limits(rows)[-1][0])
    sends = max(map(len, sent_pieces(rows)))
    halo = (HALO, 8, 128)
    out, costs = pl.pallas_call(
        functools.partial(main_kernel, rows, cells, pairs, bands),
        out_shape=(grid_type, jax.ShapeDtypeStruct((1, ITERS), jnp.float32)),
        in_specs=[vmem] * 9,
        out_specs=(vmem, smem),
        scratch_shapes=[
            tiles, pltpu.VMEM((rows * 8, 128), jnp.float32), tiles,
            rows_of(rows), rows_of(wide, (ITERS, 3)), rows_of(wide, (ITERS, 3)),
            rows_of(wide, ()), rows_of(rows),
            rows_of(rows, (ITERS, 3)), rows_of(rows, (ITERS, 3)), rows_of(rows),
            pltpu.VMEM((ITERS, 8, 128), jnp.float32), pltpu.VMEM((bands, ITERS, 8, 128), jnp.float32),
            pltpu.VMEM((2 * ITERS, 2, 3, *halo), jnp.float32), pltpu.VMEM((2 * ITERS, 2, 3, *halo), jnp.float32),
            pltpu.VMEM((128, 128), jnp.float32), pltpu.VMEM((128, 128), jnp.float32),
            dma((6,)), dma((5,)), dma((2 * ITERS, 2)), dma((2 * ITERS, 2)),
            dma((ITERS, sends)), dma((ITERS, sends)), dma((ITERS, chunks)), dma((ITERS, chunks)),
            dma((chunks,)), dma((chunks,)), dma((bands,)), dma((bands,)),
        ],
        compiler_params=pltpu.CompilerParams(
            collective_id=0, has_side_effects=True, vmem_limit_bytes=VMEM * 2**20
        ),
        name="iterations",
    )(
        as_tiles(increments), as_tiles(x_got), as_tiles(error_weight), as_tiles(depth),
        as_tiles(start_state), grid_w.reshape(3, rows, 8, 128), grid_wy.reshape(3, rows, 8, 128),
        rate, c0,
    )
    return from_tiles(out, increments.shape), costs.T


def solution(mesh):
    placed = (
        P("tm", None, "space", None),
        P(None, "space", None),
        P("space", None),
        P(None, "space", None),
        P("tm", None),
        P("tm"),
        P("tm", None),
        P("tm", None),
    )
    return jax.shard_map(
        per_device,
        mesh=mesh,
        in_specs=placed,
        out_specs=(P("tm", None, "space", None), P(None, "tm")),
        check_vma=False,
    )
```

time: 127 us -> 92.8 us (0.73)
  Pallas kernels: 109 us -> 75 us
  waiting for transfers between devices: 0.01 us -> 5.97 us
  local copies, waits for them, and re-layouts: 5.3 us -> 1.92 us
  other arithmetic: 5 us -> 2.46 us
    pallas_call x1, Pallas kernels: 37.2 us -> 13.4 us  [per_device(): pl.pallas_call(functools.partial(deposit_kernel, slots), out_shape=(grid_...]
    pallas_call x1, Pallas kernels: 71.8 us -> 61.6 us  [per_device(): pl.pallas_call(functools.partial(main_kernel, rows, cells, pairs, bands),...]
    ppermute x1, waiting for transfers between devices: 0.01 us -> 5.97 us  [per_device(): x_got = lax.ppermute(increments, both, exchange)]
    unnamed x4 -> x10, local copies, waits for them, and re-layouts: 4.03 us -> 1.68 us
  transfers between devices with their start and end apart: 2 -> 2, of which waited for: 0 -> 1; matrix products, arithmetic and copies ran while one was open for 2% -> 1% of each run, Pallas kernels for 29% -> 15%
where the time goes in v1:
time: 92.8 us; the launch traced here: 92.4 us
  Pallas kernels  75 us (81%)
  waiting for transfers between devices  5.97 us (6%)
  starting transfers between devices  5.6 us (6%)
  other arithmetic  2.46 us (3%)
  local copies, waits for them, and re-layouts  1.92 us (2%)
  between operations  1.45 us (2%)
    pallas_call x1, Pallas kernels, per_device(): pl.pallas_call(functools.partial(main_kernel, rows, cells, pairs, bands),...  61.6 us
    pallas_call x1, Pallas kernels, per_device(): pl.pallas_call(functools.partial(deposit_kernel, slots), out_shape=(grid_...  13.4 us
    ppermute x1, waiting for transfers between devices, per_device(): x_got = lax.ppermute(increments, both, exchange)  5.97 us
    ppermute x1, starting transfers between devices, per_device(): packed_got = lax.ppermute(packed, both, exchange)  3.68 us
    ppermute x1, starting transfers between devices, per_device(): x_got = lax.ppermute(increments, both, exchange)  1.92 us
  transfers between devices with their start and end apart: 2, of which 1 were waited for; matrix products, arithmetic and copies ran while one was open for 1% of the time, Pallas kernels for 15%

profile of v1, /device:TPU:129, one launch (start us, length us, event | category | flops | bytes accessed | tf_op | source)
XLA Modules:
  0.0 92.4 jit_solution(10696679324244581730)
XLA Ops:
  1.3 0.7 convert_element_type.25
  2.0 0.7 compare_select_fusion
  2.8 0.8 pad_maximum_fusion
  3.5 3.7 %collective-permute-start.1 = (f32[3,4096]{1,0:T(4,128)S(1)}, f32[3,4096]{1,0:T(4,128)S(1)}, u32[]{:S(2)}, u32[]{:S(2)}) collective-permute-start(f32[3,4096]{1,0:T(4,128)S(1)} %pad_maximum_fusion), channel_id=1, source_target_pairs={{1,4},{4,1},{3,6},{6,3},{9,12},{12,9},{11,14},{14,11},{17,20},{20,... | collective-permute-start | bytes 147464 | tf_op jit(solution)/shard_map/ppermute | solution.py:643
  7.2 1.9 %collective-permute-start = (f32[1,3,128,1024]{3,2,1,0:T(8,128)}, f32[1,3,128,1024]{3,2,1,0:T(8,128)S(1)}, u32[]{:S(2)}, u32[]{:S(2)}) collective-permute-start(f32[1,3,128,1024]{3,2,1,0:T(8,128)} %param.8), channel_id=1, source_target_pairs={{1,4},{4,1},{3,6},{6,3},{9,12},{12,9},{11,14},{14,11},{17,20},{20,... | collective-permute-start | bytes 4718600 | tf_op jit(solution)/shard_map/ppermute | solution.py:644
  9.2 0.1 negate_select_fusion.13
  9.2 0.0 collective-permute-done.1
  9.4 0.2 broadcast_in_dim.17.F
  9.7 0.0 copy-start
  9.7 0.0 copy-start.1
  9.7 0.0 copy-start.2
  9.7 0.0 copy-start.3
  9.7 13.4 %deposit.1 = (f32[3072,128]{1,0:T(8,128)S(1)}, f32[3072,128]{1,0:T(8,128)S(1)}) custom-call(s32[4096]{0:T(1024)S(1)} %fusion.6.code_ref, f32[4096]{0:T(1024)S(1)} %get-tuple-element.12.w_ref, f32[4096]{0:T(1024)S(1)} %get-tuple-element.13.wy_ref), custom_call_target="tpu_custom_call" | custom-call | flops 10000000000 | bytes 100000000 | tf_op jit(solution)/shard_map/deposit/pallas_call | solution.py:672
  23.2 6.0 %collective-permute-done = f32[1,3,128,1024]{3,2,1,0:T(8,128)S(1)} collective-permute-done((f32[1,3,128,1024]{3,2,1,0:T(8,128)}, f32[1,3,128,1024]{3,2,1,0:T(8,128)S(1)}, u32[]{:S(2)}, u32[]{:S(2)}) %collective-permute-start) | collective-permute-done | bytes 1572896 | tf_op jit(solution)/shard_map/ppermute | solution.py:644
  29.2 0.0 copy-done
  29.2 0.0 copy-done.1
  29.2 0.0 copy-done.2
  29.2 0.0 copy-done.3
  29.2 61.6 %iterations.1 = (f32[3072,128]{1,0:T(8,128)S(1)}, f32[1,2]{1,0:T(1,128)S(1)}) custom-call(f32[3072,128]{1,0:T(8,128)S(1)} %bitcast.41, f32[3072,128]{1,0:T(8,128)S(1)} %bitcast.44, f32[3072,128]{1,0:T(8,128)S(1)} %bitcast.42, f32[1024,128]{1,0:T(8,128)S(1)} %bitcast.48, f32[3072,128]{1,0:T(8,128)S(1)} %bitcast.43, f32[3,128,8,128]{3,2,1,0:T(8,128)S(1)} %bitcast.45, ...), custom_call_target="tpu_custom_call" | custom-call | tf_op jit(solution)/shard_map/iterations/pallas_call | solution.py:691
  90.8 1.1 %copy.13 = f32[1,3,128,1024]{3,2,1,0:T(8,128)} copy(f32[1,3,128,1024]{3,2,1,0:T(8,128)S(1)} %bitcast.47) | data formatting | bytes 3145728
  91.9 0.5 copy.14
  (5 shorter events, 0.2 us)
Async XLA Ops:
  3.5 5.7 %collective-permute-start.1 = (f32[3,4096]{1,0:T(4,128)S(1)}, f32[3,4096]{1,0:T(4,128)S(1)}, u32[]{:S(2)}, u32[]{:S(2)}) collective-permute-start(f32[3,4096]{1,0:T(4,128)S(1)} %pad_maximum_fusion), channel_id=1, source_target_pairs={{1,4},{4,1},{3,6},{6,3},{9,12},{12,9},{11,14},{14,11},{17,20},{20,... | collective-permute-start | bytes 147464 | tf_op jit(solution)/shard_map/ppermute | solution.py:643
  7.2 21.9 %collective-permute-start = (f32[1,3,128,1024]{3,2,1,0:T(8,128)}, f32[1,3,128,1024]{3,2,1,0:T(8,128)S(1)}, u32[]{:S(2)}, u32[]{:S(2)}) collective-permute-start(f32[1,3,128,1024]{3,2,1,0:T(8,128)} %param.8), channel_id=1, source_target_pairs={{1,4},{4,1},{3,6},{6,3},{9,12},{12,9},{11,14},{14,11},{17,20},{20,... | collective-permute-start | bytes 4718600 | tf_op jit(solution)/shard_map/ppermute | solution.py:644
  9.7 19.5 %copy-start = (f32[1,3,128,1024]{3,2,1,0:T(8,128)S(1)}, f32[1,3,128,1024]{3,2,1,0:T(8,128)}, u32[]{:S(2)}) copy-start(f32[1,3,128,1024]{3,2,1,0:T(8,128)} %param.8) | copy-start | bytes 4718596
  9.7 19.5 %copy-start.1 = (f32[3,128,1024]{2,1,0:T(8,128)S(1)}, f32[3,128,1024]{2,1,0:T(8,128)}, u32[]{:S(2)}) copy-start(f32[3,128,1024]{2,1,0:T(8,128)} %param.11) | copy-start | bytes 4718596
  9.7 19.4 %copy-start.2 = (f32[3,128,1024]{2,1,0:T(8,128)S(1)}, f32[3,128,1024]{2,1,0:T(8,128)}, u32[]{:S(2)}) copy-start(f32[3,128,1024]{2,1,0:T(8,128)} %param.9) | copy-start | bytes 4718596
  9.7 19.4 %copy-start.3 = (f32[128,1024]{1,0:T(8,128)S(1)}, f32[128,1024]{1,0:T(8,128)}, u32[]{:S(2)}) copy-start(f32[128,1024]{1,0:T(8,128)} %param.10) | copy-start | bytes 1572868

commit v2 on v1

--- a/solution.py
+++ b/solution.py
@@ -21,9 +21,9 @@
 UNROLL = 16
 VMEM = 36
 SCHEDULE = (
-    "A00", "U00", "A01", "U01", "A02", "U02", "F10", "E10", "F11",
-    "A03", "U03", "F12", "F13", "A10", "U10", "A11", "U11", "A12",
-    "U12", "F14", "E11", "A13", "U13", "A14", "U14",
+    "E00", "A00", "U00", "E01", "A01", "U01", "A02", "U02", "F10",
+    "E10", "F11", "A03", "U03", "F12", "F13", "A10", "U10", "A11",
+    "U11", "A12", "U12", "F14", "E11", "A13", "U13", "A14", "U14",
 )
 MESH = pl.DeviceIdType.MESH
 
@@ -137,6 +137,10 @@
     return plan
 
 
+def early_rows(rows):
+    return limits(rows)[0][0][1]
+
+
 def sent_pieces(rows):
     edge = rows - HALO
     plan = limits(rows)
@@ -150,9 +154,9 @@
     rows, cells, pairs, bands,
     x_own, x_got, e_own, d_own, s_own, W, WY, F, c0_ref,
     OUT, cost_ref,
-    stg_e, stg_d, stg_s, X, T, A, D, E, XN, EN, FIN, cbuf, crecv,
+    stg_r, stg_e, stg_d, stg_s, X, T, A, D, E, XN, EN, FIN, cbuf, crecv,
     edge_out, edge_in, d_top, d_bottom,
-    push_send, push_recv, halo_send, halo_recv,
+    push_send, push_recv, rest_send, rest_recv, halo_send, halo_recv,
     x_send, x_recv, e_send, e_recv, fin_send, fin_recv, c_send, c_recv,
 ):
     tm, sp, a, y, b, c, band, window = place()
@@ -175,6 +179,8 @@
     edge = jnp.where(has_top, 1.0, 0.0).astype(jnp.float32)
     plan = limits(rows)
     pieces = sent_pieces(rows)
+    part = early_rows(rows)
+    rest = rows - part
 
     edge_lines = pl.ds(pl.multiple_of(jnp.where(flip, rows * 8 - 128, 0), 128), 128)
     own_start = own & (y == 0) & (c == 0)
@@ -211,18 +217,16 @@
             0, (high - low) // size, lambda i, carry: body(low + i * size, carry), init
         )
 
-    def line_of(comp, r, j):
-        line = jnp.where(flip, (rows - 8 - r) * 8 + 7 - j, r * 8 + j)
-        return pl.ds(comp * rows * 8 + line, 8, stride=8)
-
-    def each_row(stage, comps, store):
+    def each_row(stage, comps, count, store, first=0):
         def body(r, carry):
             for comp in range(comps):
                 for j in range(8):
-                    store(comp, r + j, stage[line_of(comp, r, j), :])
+                    line = jnp.where(flip, (count - 8 - r) * 8 + 7 - j, r * 8 + j)
+                    value = stage[pl.ds(comp * count * 8 + line, 8, stride=8), :]
+                    store(comp, first + r + j, value)
             return carry
 
-        blocks(0, rows, 8, body)
+        blocks(0, count, 8, body)
 
     def store_x(comp, r, value):
         if comp == 1:
@@ -232,11 +236,11 @@
 
     @pl.when(own)
     def _():
-        each_row(x_own, 3, store_x)
+        each_row(x_own, 3, rows, store_x)
 
     @pl.when(jnp.logical_not(own))
     def _():
-        each_row(x_got, 3, store_x)
+        each_row(x_got, 3, part, store_x)
 
     pl.semaphore_wait(barrier, 2 * bands - 1 + far.astype(jnp.int32))
 
@@ -244,6 +248,21 @@
         return pltpu.make_async_remote_copy(
             src_ref=src, dst_ref=dst, send_sem=send, recv_sem=recv, device_id=to, device_id_type=MESH
         )
+
+    rest_line = pl.multiple_of(jnp.where(flip, part * 8, 0), 128)
+    rests = [
+        remote(
+            x_own.at[pl.ds(comp * rows * 8 + rest_line, rest * 8)],
+            stg_r.at[pl.ds(comp * rest * 8, rest * 8)],
+            rest_send.at[comp], rest_recv.at[comp], swap,
+        )
+        for comp in range(3)
+    ]
+
+    @pl.when(jnp.logical_not(own))
+    def _():
+        for copy in rests:
+            copy.start()
 
     push_e = remote(e_own, stg_e, push_send.at[0], push_recv.at[0], partner)
     push_d = remote(d_own, stg_d, push_send.at[1], push_recv.at[1], partner)
@@ -305,11 +324,11 @@
             for i in fresh:
                 x_copy(it, i).wait_send()
 
-    def send_x(it, low, high):
+    def send_x(it, low, high, late=None):
         @pl.when(not_first)
         def _():
             for i, (p, q) in enumerate(pieces[it]):
-                if p >= low and q <= high:
+                if p >= low and q <= high and (late is None or late == (q > part)):
                     x_copy(it, i).start()
 
     def e_copy(it, j):
@@ -354,9 +373,14 @@
         else:
             pl.when(has_top)(unpack)
 
-    send_x(0, 0, rows)
-    for side in range(2):
-        send_halo(0, side, lambda comp, r: X[comp, r])
+    send_x(0, 0, part, False)
+    send_halo(0, 0, lambda comp, r: X[comp, r])
+
+    def send_late():
+        send_x(0, 0, rows, True)
+        send_halo(0, 1, lambda comp, r: X[comp, r])
+
+    pl.when(own)(send_late)
 
     @pl.when(own)
     def _():
@@ -367,12 +391,12 @@
 
     @pl.when(own)
     def _():
-        each_row(d_own, 1, store_d)
+        each_row(d_own, 1, rows, store_d)
 
     @pl.when(jnp.logical_not(own))
     def _():
         push_d.wait_recv()
-        each_row(stg_d, 1, store_d)
+        each_row(stg_d, 1, rows, store_d)
 
 
     def edge_line(i, mirrored, line=0):
@@ -486,7 +510,15 @@
             send_halo(2 * it + 2, 1, lambda comp, r: X[comp, r])
         return acc
 
-    for j in range(len(plan[0][0])):
+    def take_rest():
+        for copy in rests:
+            copy.wait()
+        each_row(stg_r, 3, rest, store_x, part)
+        send_late()
+
+    for j, high in enumerate(plan[0][0]):
+        if j and plan[0][0][j - 1] == part:
+            pl.when(jnp.logical_not(own))(take_rest)
         run_forward(0, j)
 
     @pl.when(own)
@@ -503,8 +535,8 @@
     def store_e(comp, r, value):
         E[comp, r] = value
 
-    pl.when(own)(lambda: each_row(e_own, 3, store_e))
-    pl.when(jnp.logical_not(own))(lambda: each_row(stg_e, 3, store_e))
+    pl.when(own)(lambda: each_row(e_own, 3, rows, store_e))
+    pl.when(jnp.logical_not(own))(lambda: each_row(stg_e, 3, rows, store_e))
 
     pl.when(push_start)(lambda: push_s.wait_send())
     pl.when(need_start)(lambda: push_s.wait_recv())
@@ -515,12 +547,10 @@
         EN[0, comp, r] = value
         EN[1, comp, r] = value
 
-    pl.when(own_start)(lambda: each_row(s_own, 3, store_s))
-    pl.when(need_start)(lambda: each_row(stg_s, 3, store_s))
+    pl.when(own_start)(lambda: each_row(s_own, 3, rows, store_s))
+    pl.when(need_start)(lambda: each_row(stg_s, 3, rows, store_s))
 
     acc = [0.5 * c0_ref[...] for _ in range(ITERS)]
-    send_edge(0, 0)
-    send_edge(0, 1)
     for token in SCHEDULE:
         kind, it, j = token[0], int(token[1]), int(token[2])
         if kind == "F":
@@ -641,7 +671,9 @@
     )
     packed = lax.optimization_barrier(packed)
     packed_got = lax.ppermute(packed, both, exchange)
-    x_got = lax.ppermute(increments, both, exchange)
+    early = early_rows(rows)
+    x_early = jnp.where(a == 1, increments[:, :, :early], increments[:, :, rows - early :])
+    x_got = lax.ppermute(x_early, both, exchange)
     packed = jnp.where(own, packed, packed_got)
 
     index = packed[0].astype(jnp.int32)
@@ -694,6 +726,7 @@
         in_specs=[vmem] * 9,
         out_specs=(vmem, smem),
         scratch_shapes=[
+            pltpu.VMEM((3 * (rows - early) * 8, 128), jnp.float32),
             tiles, pltpu.VMEM((rows * 8, 128), jnp.float32), tiles,
             rows_of(rows), rows_of(wide, (ITERS, 3)), rows_of(wide, (ITERS, 3)),
             rows_of(wide, ()), rows_of(rows),
@@ -701,7 +734,7 @@
             pltpu.VMEM((ITERS, 8, 128), jnp.float32), pltpu.VMEM((bands, ITERS, 8, 128), jnp.float32),
             pltpu.VMEM((2 * ITERS, 2, 3, *halo), jnp.float32), pltpu.VMEM((2 * ITERS, 2, 3, *halo), jnp.float32),
             pltpu.VMEM((128, 128), jnp.float32), pltpu.VMEM((128, 128), jnp.float32),
-            dma((6,)), dma((5,)), dma((2 * ITERS, 2)), dma((2 * ITERS, 2)),
+            dma((6,)), dma((5,)), dma((3,)), dma((3,)), dma((2 * ITERS, 2)), dma((2 * ITERS, 2)),
             dma((ITERS, sends)), dma((ITERS, sends)), dma((ITERS, chunks)), dma((ITERS, chunks)),
             dma((chunks,)), dma((chunks,)), dma((bands,)), dma((bands,)),
         ],

time: 92.8 us -> 92.8 us (level)
  waiting for transfers between devices: 5.97 us -> 0.01 us
  Pallas kernels: 75 us -> 79.1 us
  other arithmetic: 2.46 us -> 4.09 us
    ppermute x1, waiting for transfers between devices: 5.97 us -> 0.01 us  [per_device(): x_got = lax.ppermute(x_early, both, exchange)]
    pallas_call x1, Pallas kernels: 61.6 us -> 65.6 us  [per_device(): pl.pallas_call(functools.partial(main_kernel, rows, cells, pairs, bands),...]
    select_n x0 -> x1, other arithmetic: none -> 1.63 us  [per_device(): jnp.where(a == 1, increments[:, :, :early], increments[:, :, rows - early:])]
  transfers between devices with their start and end apart: 2 -> 2, of which waited for: 1 -> 0; matrix products, arithmetic and copies ran while one was open for 1% -> 2% of each run, Pallas kernels for 15% -> 15%
where the time goes in v2:
time: 92.8 us; the launch traced here: 92.2 us
  Pallas kernels  79.1 us (85%)
  starting transfers between devices  5.6 us (6%)
  other arithmetic  4.09 us (4%)
  local copies, waits for them, and re-layouts  1.92 us (2%)
  between operations  1.49 us (2%)
    pallas_call x1, Pallas kernels, per_device(): pl.pallas_call(functools.partial(main_kernel, rows, cells, pairs, bands),...  65.6 us
    pallas_call x1, Pallas kernels, per_device(): pl.pallas_call(functools.partial(deposit_kernel, slots), out_shape=(grid_...  13.4 us
    ppermute x1, starting transfers between devices, per_device(): packed_got = lax.ppermute(packed, both, exchange)  3.68 us
    ppermute x1, starting transfers between devices, per_device(): x_got = lax.ppermute(x_early, both, exchange)  1.92 us
  transfers between devices with their start and end apart: 2, of which 0 were waited for; matrix products, arithmetic and copies ran while one was open for 2% of the time, Pallas kernels for 15%

profile of v2, /device:TPU:129, one launch (start us, length us, event | category | flops | bytes accessed | tf_op | source)
XLA Modules:
  0.0 92.2 jit_solution(125831944757482385)
XLA Ops:
  1.3 0.7 convert_element_type.25
  2.0 0.7 compare_select_fusion
  2.8 0.8 pad_maximum_fusion
  3.5 3.7 %collective-permute-start.1 = (f32[3,4096]{1,0:T(4,128)S(1)}, f32[3,4096]{1,0:T(4,128)S(1)}, u32[]{:S(2)}, u32[]{:S(2)}) collective-permute-start(f32[3,4096]{1,0:T(4,128)S(1)} %pad_maximum_fusion), channel_id=1, source_target_pairs={{1,4},{4,1},{3,6},{6,3},{9,12},{12,9},{11,14},{14,11},{17,20},{20,... | collective-permute-start | bytes 147464 | tf_op jit(solution)/shard_map/ppermute | solution.py:673
  7.2 1.6 %slice_select_fusion = f32[1,3,80,1024]{3,2,1,0:T(8,128)S(1)} fusion(f32[1,3,128,1024]{3,2,1,0:T(8,128)} %param.8, pred[]{:T(512)S(6)} %eq.17), kind=kLoop, calls=%fused_computation | loop fusion | flops 245760 | bytes 2949121 | tf_op jit(solution)/shard_map/jit(_where)/select_n | solution.py:675
  8.9 1.9 %collective-permute-start = (f32[1,3,80,1024]{3,2,1,0:T(8,128)S(1)}, f32[1,3,80,1024]{3,2,1,0:T(8,128)S(1)}, u32[]{:S(2)}, u32[]{:S(2)}) collective-permute-start(f32[1,3,80,1024]{3,2,1,0:T(8,128)S(1)} %slice_select_fusion), channel_id=1, source_target_pairs={{1,4},{4,1},{3,6},{6,3},{9,12},{12,9},{11,14},{14,11},{17,20},{20,... | collective-permute-start | bytes 2949128 | tf_op jit(solution)/shard_map/ppermute | solution.py:676
  10.8 0.1 negate_select_fusion.13
  10.9 0.0 collective-permute-done.1
  11.1 0.2 broadcast_in_dim.17.F
  11.3 0.0 copy-start
  11.3 0.0 copy-start.1
  11.4 0.0 copy-start.2
  11.4 0.0 copy-start.3
  11.4 13.4 %deposit.1 = (f32[3072,128]{1,0:T(8,128)S(1)}, f32[3072,128]{1,0:T(8,128)S(1)}) custom-call(s32[4096]{0:T(1024)S(1)} %fusion.6.code_ref, f32[4096]{0:T(1024)S(1)} %get-tuple-element.12.w_ref, f32[4096]{0:T(1024)S(1)} %get-tuple-element.13.wy_ref), custom_call_target="tpu_custom_call" | custom-call | flops 10000000000 | bytes 100000000 | tf_op jit(solution)/shard_map/deposit/pallas_call | solution.py:704
  24.8 0.0 collective-permute-done
  24.8 0.0 copy-done
  24.8 0.0 copy-done.1
  24.9 0.0 copy-done.2
  24.9 0.0 copy-done.3
  24.9 65.6 %iterations.1 = (f32[3072,128]{1,0:T(8,128)S(1)}, f32[1,2]{1,0:T(1,128)S(1)}) custom-call(f32[3072,128]{1,0:T(8,128)S(1)} %bitcast.41, f32[1920,128]{1,0:T(8,128)S(1)} %bitcast.47, f32[3072,128]{1,0:T(8,128)S(1)} %bitcast.42, f32[1024,128]{1,0:T(8,128)S(1)} %bitcast.48, f32[3072,128]{1,0:T(8,128)S(1)} %bitcast.43, f32[3,128,8,128]{3,2,1,0:T(8,128)S(1)} %bitcast.44, ...), custom_call_target="tpu_custom_call" | custom-call | tf_op jit(solution)/shard_map/iterations/pallas_call | solution.py:723
  90.5 1.1 %copy.13 = f32[1,3,128,1024]{3,2,1,0:T(8,128)} copy(f32[1,3,128,1024]{3,2,1,0:T(8,128)S(1)} %bitcast.46) | data formatting | bytes 3145728
  91.7 0.5 copy.14
  (5 shorter events, 0.2 us)
Async XLA Ops:
  3.5 7.4 %collective-permute-start.1 = (f32[3,4096]{1,0:T(4,128)S(1)}, f32[3,4096]{1,0:T(4,128)S(1)}, u32[]{:S(2)}, u32[]{:S(2)}) collective-permute-start(f32[3,4096]{1,0:T(4,128)S(1)} %pad_maximum_fusion), channel_id=1, source_target_pairs={{1,4},{4,1},{3,6},{6,3},{9,12},{12,9},{11,14},{14,11},{17,20},{20,... | collective-permute-start | bytes 147464 | tf_op jit(solution)/shard_map/ppermute | solution.py:673
  8.9 16.0 %collective-permute-start = (f32[1,3,80,1024]{3,2,1,0:T(8,128)S(1)}, f32[1,3,80,1024]{3,2,1,0:T(8,128)S(1)}, u32[]{:S(2)}, u32[]{:S(2)}) collective-permute-start(f32[1,3,80,1024]{3,2,1,0:T(8,128)S(1)} %slice_select_fusion), channel_id=1, source_target_pairs={{1,4},{4,1},{3,6},{6,3},{9,12},{12,9},{11,14},{14,11},{17,20},{20,... | collective-permute-start | bytes 2949128 | tf_op jit(solution)/shard_map/ppermute | solution.py:676
  11.3 13.5 %copy-start = (f32[1,3,128,1024]{3,2,1,0:T(8,128)S(1)}, f32[1,3,128,1024]{3,2,1,0:T(8,128)}, u32[]{:S(2)}) copy-start(f32[1,3,128,1024]{3,2,1,0:T(8,128)} %param.8) | copy-start | bytes 4718596
  11.3 13.5 %copy-start.1 = (f32[3,128,1024]{2,1,0:T(8,128)S(1)}, f32[3,128,1024]{2,1,0:T(8,128)}, u32[]{:S(2)}) copy-start(f32[3,128,1024]{2,1,0:T(8,128)} %param.11) | copy-start | bytes 4718596
  11.4 13.5 %copy-start.2 = (f32[3,128,1024]{2,1,0:T(8,128)S(1)}, f32[3,128,1024]{2,1,0:T(8,128)}, u32[]{:S(2)}) copy-start(f32[3,128,1024]{2,1,0:T(8,128)} %param.9) | copy-start | bytes 4718596
  11.4 13.5 %copy-start.3 = (f32[128,1024]{1,0:T(8,128)S(1)}, f32[128,1024]{1,0:T(8,128)}, u32[]{:S(2)}) copy-start(f32[128,1024]{1,0:T(8,128)} %param.10) | copy-start | bytes 1572868

commit v3 on v2

--- a/solution.py
+++ b/solution.py
@@ -21,7 +21,7 @@
 UNROLL = 16
 VMEM = 36
 SCHEDULE = (
-    "E00", "A00", "U00", "E01", "A01", "U01", "A02", "U02", "F10",
+    "A00", "U00", "A01", "U01", "A02", "U02", "F10",
     "E10", "F11", "A03", "U03", "F12", "F13", "A10", "U10", "A11",
     "U11", "A12", "U12", "F14", "E11", "A13", "U13", "A14", "U14",
 )
@@ -519,7 +519,8 @@
     for j, high in enumerate(plan[0][0]):
         if j and plan[0][0][j - 1] == part:
             pl.when(jnp.logical_not(own))(take_rest)
-        run_forward(0, j)
+        if high < rows:
+            run_forward(0, j)
 
     @pl.when(own)
     def _():
@@ -537,6 +538,9 @@
 
     pl.when(own)(lambda: each_row(e_own, 3, rows, store_e))
     pl.when(jnp.logical_not(own))(lambda: each_row(stg_e, 3, rows, store_e))
+    send_edge(0, 0)
+    run_forward(0, len(plan[0][0]) - 1)
+    send_edge(0, 1)
 
     pl.when(push_start)(lambda: push_s.wait_send())
     pl.when(need_start)(lambda: push_s.wait_recv())

time: 92.8 us -> 88 us (0.948)
  Pallas kernels: 79.1 us -> 74.5 us
    pallas_call x1, Pallas kernels: 65.6 us -> 61.1 us  [per_device(): pl.pallas_call(functools.partial(main_kernel, rows, cells, pairs, bands),...]
where the time goes in v3:
time: 88 us; the launch traced here: 87.6 us
  Pallas kernels  74.5 us (85%)
  starting transfers between devices  5.6 us (6%)
  other arithmetic  4.09 us (5%)
  local copies, waits for them, and re-layouts  1.92 us (2%)
  between operations  1.49 us (2%)
    pallas_call x1, Pallas kernels, per_device(): pl.pallas_call(functools.partial(main_kernel, rows, cells, pairs, bands),...  61.1 us
    pallas_call x1, Pallas kernels, per_device(): pl.pallas_call(functools.partial(deposit_kernel, slots), out_shape=(grid_...  13.4 us
    ppermute x1, starting transfers between devices, per_device(): packed_got = lax.ppermute(packed, both, exchange)  3.68 us
    ppermute x1, starting transfers between devices, per_device(): x_got = lax.ppermute(x_early, both, exchange)  1.92 us
  transfers between devices with their start and end apart: 2, of which 0 were waited for; matrix products, arithmetic and copies ran while one was open for 2% of the time, Pallas kernels for 15%

profile of v3, /device:TPU:129, one launch (start us, length us, event | category | flops | bytes accessed | tf_op | source)
XLA Modules:
  0.0 87.6 jit_solution(12295113942427259237)
XLA Ops:
  1.3 0.7 convert_element_type.25
  2.0 0.7 compare_select_fusion
  2.8 0.8 pad_maximum_fusion
  3.5 3.7 %collective-permute-start.1 = (f32[3,4096]{1,0:T(4,128)S(1)}, f32[3,4096]{1,0:T(4,128)S(1)}, u32[]{:S(2)}, u32[]{:S(2)}) collective-permute-start(f32[3,4096]{1,0:T(4,128)S(1)} %pad_maximum_fusion), channel_id=1, source_target_pairs={{1,4},{4,1},{3,6},{6,3},{9,12},{12,9},{11,14},{14,11},{17,20},{20,... | collective-permute-start | bytes 147464 | tf_op jit(solution)/shard_map/ppermute | solution.py:677
  7.2 1.6 %slice_select_fusion = f32[1,3,80,1024]{3,2,1,0:T(8,128)S(1)} fusion(f32[1,3,128,1024]{3,2,1,0:T(8,128)} %param.8, pred[]{:T(512)S(6)} %eq.17), kind=kLoop, calls=%fused_computation | loop fusion | flops 245760 | bytes 2949121 | tf_op jit(solution)/shard_map/jit(_where)/select_n | solution.py:679
  8.9 1.9 %collective-permute-start = (f32[1,3,80,1024]{3,2,1,0:T(8,128)S(1)}, f32[1,3,80,1024]{3,2,1,0:T(8,128)S(1)}, u32[]{:S(2)}, u32[]{:S(2)}) collective-permute-start(f32[1,3,80,1024]{3,2,1,0:T(8,128)S(1)} %slice_select_fusion), channel_id=1, source_target_pairs={{1,4},{4,1},{3,6},{6,3},{9,12},{12,9},{11,14},{14,11},{17,20},{20,... | collective-permute-start | bytes 2949128 | tf_op jit(solution)/shard_map/ppermute | solution.py:680
  10.8 0.1 negate_select_fusion.13
  10.9 0.0 collective-permute-done.1
  11.1 0.2 broadcast_in_dim.17.F
  11.3 0.0 copy-start
  11.3 0.0 copy-start.1
  11.4 0.0 copy-start.2
  11.4 0.0 copy-start.3
  11.4 13.4 %deposit.1 = (f32[3072,128]{1,0:T(8,128)S(1)}, f32[3072,128]{1,0:T(8,128)S(1)}) custom-call(s32[4096]{0:T(1024)S(1)} %fusion.6.code_ref, f32[4096]{0:T(1024)S(1)} %get-tuple-element.12.w_ref, f32[4096]{0:T(1024)S(1)} %get-tuple-element.13.wy_ref), custom_call_target="tpu_custom_call" | custom-call | flops 10000000000 | bytes 100000000 | tf_op jit(solution)/shard_map/deposit/pallas_call | solution.py:708
  24.8 0.0 collective-permute-done
  24.8 0.0 copy-done
  24.8 0.0 copy-done.1
  24.9 0.0 copy-done.2
  24.9 0.0 copy-done.3
  24.9 61.1 %iterations.1 = (f32[3072,128]{1,0:T(8,128)S(1)}, f32[1,2]{1,0:T(1,128)S(1)}) custom-call(f32[3072,128]{1,0:T(8,128)S(1)} %bitcast.41, f32[1920,128]{1,0:T(8,128)S(1)} %bitcast.47, f32[3072,128]{1,0:T(8,128)S(1)} %bitcast.42, f32[1024,128]{1,0:T(8,128)S(1)} %bitcast.48, f32[3072,128]{1,0:T(8,128)S(1)} %bitcast.43, f32[3,128,8,128]{3,2,1,0:T(8,128)S(1)} %bitcast.44, ...), custom_call_target="tpu_custom_call" | custom-call | tf_op jit(solution)/shard_map/iterations/pallas_call | solution.py:727
  86.0 1.1 %copy.13 = f32[1,3,128,1024]{3,2,1,0:T(8,128)} copy(f32[1,3,128,1024]{3,2,1,0:T(8,128)S(1)} %bitcast.46) | data formatting | bytes 3145728
  87.1 0.5 copy.14
  (5 shorter events, 0.2 us)
Async XLA Ops:
  3.5 7.4 %collective-permute-start.1 = (f32[3,4096]{1,0:T(4,128)S(1)}, f32[3,4096]{1,0:T(4,128)S(1)}, u32[]{:S(2)}, u32[]{:S(2)}) collective-permute-start(f32[3,4096]{1,0:T(4,128)S(1)} %pad_maximum_fusion), channel_id=1, source_target_pairs={{1,4},{4,1},{3,6},{6,3},{9,12},{12,9},{11,14},{14,11},{17,20},{20,... | collective-permute-start | bytes 147464 | tf_op jit(solution)/shard_map/ppermute | solution.py:677
  8.9 16.0 %collective-permute-start = (f32[1,3,80,1024]{3,2,1,0:T(8,128)S(1)}, f32[1,3,80,1024]{3,2,1,0:T(8,128)S(1)}, u32[]{:S(2)}, u32[]{:S(2)}) collective-permute-start(f32[1,3,80,1024]{3,2,1,0:T(8,128)S(1)} %slice_select_fusion), channel_id=1, source_target_pairs={{1,4},{4,1},{3,6},{6,3},{9,12},{12,9},{11,14},{14,11},{17,20},{20,... | collective-permute-start | bytes 2949128 | tf_op jit(solution)/shard_map/ppermute | solution.py:680
  11.3 13.5 %copy-start = (f32[1,3,128,1024]{3,2,1,0:T(8,128)S(1)}, f32[1,3,128,1024]{3,2,1,0:T(8,128)}, u32[]{:S(2)}) copy-start(f32[1,3,128,1024]{3,2,1,0:T(8,128)} %param.8) | copy-start | bytes 4718596
  11.3 13.5 %copy-start.1 = (f32[3,128,1024]{2,1,0:T(8,128)S(1)}, f32[3,128,1024]{2,1,0:T(8,128)}, u32[]{:S(2)}) copy-start(f32[3,128,1024]{2,1,0:T(8,128)} %param.11) | copy-start | bytes 4718596
  11.4 13.5 %copy-start.2 = (f32[3,128,1024]{2,1,0:T(8,128)S(1)}, f32[3,128,1024]{2,1,0:T(8,128)}, u32[]{:S(2)}) copy-start(f32[3,128,1024]{2,1,0:T(8,128)} %param.9) | copy-start | bytes 4718596
  11.4 13.5 %copy-start.3 = (f32[128,1024]{1,0:T(8,128)S(1)}, f32[128,1024]{1,0:T(8,128)}, u32[]{:S(2)}) copy-start(f32[128,1024]{1,0:T(8,128)} %param.10) | copy-start | bytes 1572868
